TPU v7x, 256 devices: a whole 4x4x8 slice. The times are simulated.
256 devices in a mesh: dp: 16 (over y, x), sp: 8 (over z), shift: 2 (over core).
Axes of the slice: x: 4, y: 4, z: 8, core: 2. Of those that a mesh axis runs over, the one named last changes fastest.
Arguments:
- query_rows: bfloat16 [32, 2048, 32, 128], P(('shift', 'dp'), 'sp'), parts along dimension 0, may hold values from -6 to 6
- key_rows: bfloat16 [32, 2048, 32, 128], P(('shift', 'dp'), 'sp'), parts along dimension 0, may hold values from -6 to 6
- value_rows: bfloat16 [32, 2048, 32, 128], P(('shift', 'dp'), 'sp'), parts along dimension 0, may hold values from -6 to 6
- out_weight: bfloat16 [8192, 4096], P(('shift', 'dp')), parts along dimension 0, may hold values from -0.09375 to 0.09375
Outputs:
- mixer_out: bfloat16 [32, 2048, 4096], P(('shift', 'dp'), 'sp'), parts along dimension 0
There are 2 independent parts, one for each index of `shift`. A program takes and returns all parts, laid end to end along the dimension named above; each array names one. Nothing has to cross between parts.
All inputs are finite; a program needn't handle non-finite values.
Results may differ from a plain program's by a relative error of at most 0.006.
Values may be sent and summed in bfloat16 or wider, within the bound.
A program may use at most 128 MiB of HBM per device.

v0:
```python
import jax
import jax.numpy as jnp
from jax import lax
from jax.sharding import PartitionSpec as P


def feature_map(values):
    wide = values.astype(jnp.float32)
    return jnp.where(wide > 0.0, wide + 1.0, jnp.exp(jnp.minimum(wide, 0.0))).astype(jnp.bfloat16)


def finish_heads(read, count):
    result = read * count**0.5
    return result.astype(jnp.bfloat16)


def ask_state(features, state, mass):
    top = jnp.einsum(
        "bthd,bhde->bthe", features, state.astype(jnp.bfloat16), preferred_element_type=jnp.float32
    )
    bottom = jnp.einsum(
        "bthd,bhd->bth", features.astype(jnp.float32), mass, precision=lax.Precision.HIGHEST
    )
    return top / (bottom + 0.001)[..., None]


def body(query_rows, key_rows, value_rows, out_weight):
    query_feature, key_feature = (feature_map(query_rows), feature_map(key_rows))
    count = query_rows.shape[1] * lax.axis_size("sp")
    part_state = jnp.einsum(
        "bthd,bthe->bhde", key_feature, value_rows, preferred_element_type=jnp.float32
    )
    part_mass = jnp.sum(key_feature.astype(jnp.float32), axis=1)
    state, mass = lax.psum((part_state, part_mass), "sp")
    read = ask_state(query_feature, state / count, mass / count)
    mixed = finish_heads(read, count)
    mixed = mixed.reshape(mixed.shape[0], mixed.shape[1], -1)
    return jnp.einsum(
        "btw,wv->btv",
        mixed,
        lax.all_gather(out_weight, "dp", axis=0, tiled=True),
        preferred_element_type=jnp.float32,
    ).astype(jnp.bfloat16)


def solution(mesh):
    placed = (
        P(("shift", "dp"), "sp", None, None),
        P(("shift", "dp"), "sp", None, None),
        P(("shift", "dp"), "sp", None, None),
        P(("shift", "dp"), None),
    )
    return jax.shard_map(
        body, mesh=mesh, in_specs=placed, out_specs=P(("shift", "dp"), "sp", None), check_vma=False
    )
```

profile of v0, /device:TPU:1, one launch (start us, length us, event | category | flops | bytes accessed | tf_op | source)
XLA Modules:
  0.0 245.8 jit_solution(8136283110599534945)
XLA Ops:
  7.4 0.0 copy-start
  7.4 0.0 all-reduce.2.cloned.1.call-start
  7.4 3.0 %fusion.21 = (bf16[256,32,128]{2,1,0:T(8,128)(2,1)S(1)}, f32[32,128]{1,0:T(8,128)S(1)}) fusion(bf16[1,256,32,128]{3,2,1,0:T(8,128)(2,1)} %param.5), kind=kLoop, calls=%fused_computation.26 | loop fusion | flops 8384512 | bytes 4210688 | tf_op jit(solution)/shard_map/reshape
  10.3 0.0 copy-done
  10.3 3.0 %fusion.13 = f32[1,32,128,128]{3,2,1,0:T(8,128)} fusion(bf16[256,32,128]{2,1,0:T(8,128)(2,1)S(1)} %bitcast.41, bf16[256,32,128]{2,1,0:T(8,128)(2,1)S(1)} %get-tuple-element.5), kind=kOutput, calls=%fused_computation.23 | convolution fusion | flops 268435456 | bytes 6291456 | tf_op jit(solution)/shard_map/bthd,bthe->bhde/dot_general | solution.py:30
  13.4 0.0 all-reduce.2.cloned.1.call-update
  13.4 0.0 all-gather.2.cloned.1.call-start
  13.4 0.5 all-gather.2.cloned.1.call-update
  14.0 4.0 %fusion.9 = bf16[256,32,128]{2,1,0:T(8,128)(2,1)} fusion(bf16[1,256,32,128]{3,2,1,0:T(8,128)(2,1)} %param.4), kind=kLoop, calls=%fused_computation.18 | loop fusion | flops 6291456 | bytes 4194304 | tf_op jit(solution)/shard_map/reshape.5
  18.0 4.3 %copy.11 = bf16[256,32,128]{0,2,1:T(8,128)(2,1)} copy(bf16[256,32,128]{2,1,0:T(8,128)(2,1)} %fusion.9) | data formatting | bytes 4194304 | tf_op jit(solution)/shard_map/reshape.5
  22.3 29.3 %psum.15 = f32[1,32,128]{2,1,0:T(8,128)S(1)} all-reduce(f32[1,32,128]{2,1,0:T(8,128)S(1)} %bitcast.43), channel_id=1, replica_groups=mesh['dp'=16,'sp'=8,'shift'=2] {'sp'}, use_global_device_ids=true, to_apply=%region_2.3 | all-reduce | flops 4096 | bytes 32768 | tf_op jit(solution)/shard_map/psum | solution.py:34
  51.6 2.5 %fusion.24 = f32[32,1,256]{2,1,0:T(1,128)S(1)} fusion(f32[32,128,1]{1,2,0:T(1,128)S(1)} %bitcast.44, bf16[256,32,128]{0,2,1:T(8,128)(2,1)} %copy.11), kind=kOutput, calls=%fused_computation.31 | convolution fusion | flops 12582912 | bytes 2146304 | tf_op jit(solution)/shard_map/bthd,bhd->bth/dot_general | solution.py:21
  54.1 41.6 %all-reduce.2.cloned.1.call-done = f32[1,32,128,128]{3,2,1,0:T(8,128)} async-done(((f32[1,32,128,128]{3,2,1,0:T(8,128)}), f32[1,32,128,128]{3,2,1,0:T(8,128)}) %all-reduce.2.cloned.1.call-update) | async-done | bytes 2097168 | tf_op jit(solution)/shard_map/psum | solution.py:34
  95.7 4.3 %fusion.8 = bf16[1,256,32,128]{1,3,2,0:T(8,128)(2,1)} fusion(bf16[256,32,128]{0,2,1:T(8,128)(2,1)} %copy.11, f32[256,32]{0,1:T(8,128)S(1)} %fusion.22, f32[1,32,128,128]{3,2,1,0:T(8,128)} %all-reduce.2.cloned.1.call-done), kind=kOutput, calls=%fused_computation.16 | convolution fusion | flops 272629760 | bytes 6324224 | tf_op jit(solution)/shard_map/bthd,bhde->bthe/dot_general | solution.py:18
  100.0 121.8 %all-gather.2.cloned.1.call-done = bf16[4096,4096]{1,0:T(8,128)(2,1)} async-done(((bf16[256,4096]{1,0:T(8,128)(2,1)}), bf16[4096,4096]{1,0:T(8,128)(2,1)}) %all-gather.2.cloned.1.call-update) | async-done | bytes 33554448 | tf_op jit(solution)/shard_map/all_gather | solution.py:41
  221.8 16.6 %fusion = bf16[1,256,4096]{2,1,0:T(8,128)(2,1)} fusion(bf16[256,4096]{0,1:T(8,128)(2,1)} %bitcast.42, bf16[4096,4096]{1,0:T(8,128)(2,1)} %all-gather.2.cloned.1.call-done), kind=kOutput, calls=%fused_computation.7 | convolution fusion | flops 8590983168 | bytes 37748736 | tf_op jit(solution)/shard_map/btw,wv->btv/dot_general | solution.py:38
  (2 shorter events, 0.0 us)
Async XLA Ops:
  7.4 3.0 %copy-start = (bf16[1,256,32,128]{3,2,1,0:T(8,128)(2,1)S(1)}, bf16[1,256,32,128]{3,2,1,0:T(8,128)(2,1)}, u32[]{:S(2)}) copy-start(bf16[1,256,32,128]{3,2,1,0:T(8,128)(2,1)} %param.6) | copy-start | bytes 6291460
  7.4 88.3 %all-reduce.2.cloned.1.call-start = ((), (), s32[]{:S(2)}) async-start(), calls=%async_computation | async-start | bytes 4194304 | tf_op jit(solution)/shard_map/psum | solution.py:34
  13.4 208.4 %all-gather.2.cloned.1.call-start = ((), (), s32[]{:S(2)}) async-start(), calls=%async_computation.1 | async-start | bytes 35651584 | tf_op jit(solution)/shard_map/all_gather | solution.py:41
Sparse Core Ops, SparseCore 0:
  13.5 82.1 all-reduce.1
Sparse Core Ops, SparseCore 1:
  16.3 205.4 all-gather.1
where the time goes:
time: 246 us
  waiting for transfers between devices  164 us (67%)
  blocking collectives  29.3 us (12%)
  matrix products  26.4 us (11%)
  between operations  14.9 us (6%)
  other arithmetic  6.97 us (3%)
  local copies, waits for them, and re-layouts  4.31 us (2%)
    all_gather x1, waiting for transfers between devices, body(): lax.all_gather(out_weight, 'dp', axis=0, tiled=True)  122 us
    psum x1, waiting for transfers between devices, body(): state, mass = lax.psum((part_state, part_mass), 'sp')  41.6 us
    psum x1, blocking collectives, body(): state, mass = lax.psum((part_state, part_mass), 'sp')  29.3 us
    dot_general x1, matrix products, body(): jnp.einsum('btw,wv->btv', mixed, lax.all_gather(out_weight, 'dp', axis=0,...  16.6 us
  transfers between devices with their start and end apart: 2, of which 2 were waited for; matrix products, arithmetic and copies ran while one was open for 6% of the time, Pallas kernels for 0%

commit v1 on v0

--- a/solution.py
+++ b/solution.py
@@ -2,6 +2,22 @@
 import jax.numpy as jnp
 from jax import lax
 from jax.sharding import PartitionSpec as P
+
+
+def summed_both_ways(shard, axis, dim, product):
+    size, here, rows = (lax.axis_size(axis), lax.axis_index(axis), shard.shape[dim])
+    right = [(i, (i + 1) % size) for i in range(size)]
+    left = [(i, (i - 1) % size) for i in range(size)]
+    halfway = size // 2
+    from_left = from_right = shard
+    running = product(shard, here * rows)
+    for step in range(1, halfway + 1):
+        from_left = lax.ppermute(from_left, axis, right)
+        if step < size - halfway:
+            from_right = lax.ppermute(from_right, axis, left)
+            running = running + product(from_right, (here + step) % size * rows)
+        running = running + product(from_left, (here - step) % size * rows)
+    return running
 
 
 def feature_map(values):
@@ -35,11 +51,16 @@
     read = ask_state(query_feature, state / count, mass / count)
     mixed = finish_heads(read, count)
     mixed = mixed.reshape(mixed.shape[0], mixed.shape[1], -1)
-    return jnp.einsum(
-        "btw,wv->btv",
-        mixed,
-        lax.all_gather(out_weight, "dp", axis=0, tiled=True),
-        preferred_element_type=jnp.float32,
+    return summed_both_ways(
+        out_weight,
+        "dp",
+        0,
+        lambda shard, at: jnp.einsum(
+            "btw,wv->btv",
+            lax.dynamic_slice_in_dim(mixed, at, shard.shape[0], axis=2),
+            shard,
+            preferred_element_type=jnp.float32,
+        ),
     ).astype(jnp.bfloat16)
 
 

time: 246 us -> 400 us (1.63)
  the two profiles are of different devices: /device:TPU:1 before, /device:TPU:128 now
where the time goes in v1:
time: 400 us
  waiting for transfers between devices  280 us (70%)
  starting transfers between devices  37.8 us (9%)
  matrix products  29.8 us (7%)
  blocking collectives  27.9 us (7%)
  between operations  13.7 us (3%)
  local copies, waits for them, and re-layouts  5.48 us (1%)
  other arithmetic  5.23 us (1%)
    ppermute x8, waiting for transfers between devices, summed_both_ways(): from_left = lax.ppermute(from_left, axis, right)  210 us
    ppermute x7, waiting for transfers between devices, summed_both_ways(): from_right = lax.ppermute(from_right, axis, left)  69.9 us
    ppermute x7, starting transfers between devices, summed_both_ways(): from_right = lax.ppermute(from_right, axis, left)  36.2 us
    psum x1, blocking collectives, body(): state, mass = lax.psum((part_state, part_mass), 'sp')  27.9 us
    dot_general x16, matrix products, body(): jnp.einsum('btw,wv->btv', lax.dynamic_slice_in_dim(mixed, at, shard.shape...  23.3 us
  transfers between devices with their start and end apart: 16, of which 11 were waited for; matrix products, arithmetic and copies ran while one was open for 9% of the time, Pallas kernels for 0%

profile of v1, /device:TPU:128, one launch (start us, length us, event | category | flops | bytes accessed | tf_op | source)
XLA Modules:
  0.0 399.5 jit_solution(12538098169008944301)
XLA Ops:
  6.5 0.0 copy-start
  6.5 0.0 all-reduce.2.cloned.1.call-start
  6.5 1.5 collective-permute-start.1
  8.0 3.9 collective-permute-start
  11.9 45.7 %collective-permute-done.1 = bf16[256,4096]{1,0:T(8,128)(2,1)S(1)} collective-permute-done((bf16[256,4096]{1,0:T(8,128)(2,1)}, bf16[256,4096]{1,0:T(8,128)(2,1)S(1)}, u32[]{:S(2)}, u32[]{:S(2)}) %collective-permute-start.1) | collective-permute-done | bytes 2097184 | tf_op jit(solution)/shard_map/ppermute | solution.py:15
  57.6 0.0 collective-permute-start.3
  57.6 0.0 collective-permute-done
  57.6 0.0 copy-start.10
  57.6 5.3 %collective-permute-start.2 = (bf16[256,4096]{1,0:T(8,128)(2,1)S(1)}, bf16[256,4096]{1,0:T(8,128)(2,1)S(1)}, u32[]{:S(2)}, u32[]{:S(2)}) collective-permute-start(bf16[256,4096]{1,0:T(8,128)(2,1)S(1)} %collective-permute-done), channel_id=1, source_target_pairs={{0,240},{16,0},{32,16},{48,32},{64,48},{80,64},{96,80},{112,96},{1... | collective-permute-start | bytes 6291464 | tf_op jit(solution)/shard_map/ppermute | solution.py:17
  62.9 44.6 %collective-permute-done.3 = bf16[256,4096]{1,0:T(8,128)(2,1)S(1)} collective-permute-done((bf16[256,4096]{1,0:T(8,128)(2,1)S(1)}, bf16[256,4096]{1,0:T(8,128)(2,1)S(1)}, u32[]{:S(2)}, u32[]{:S(2)}) %collective-permute-start.3) | collective-permute-done | bytes 2097184 | tf_op jit(solution)/shard_map/ppermute | solution.py:15
  107.6 0.0 collective-permute-start.5
  107.6 0.0 collective-permute-done.2
  107.6 0.0 copy-start.8
  107.6 5.3 %collective-permute-start.4 = (bf16[256,4096]{1,0:T(8,128)(2,1)S(1)}, bf16[256,4096]{1,0:T(8,128)(2,1)}, u32[]{:S(2)}, u32[]{:S(2)}) collective-permute-start(bf16[256,4096]{1,0:T(8,128)(2,1)S(1)} %collective-permute-done.2), channel_id=1, source_target_pairs={{0,240},{16,0},{32,16},{48,32},{64,48},{80,64},{96,80},{112,96},{1... | collective-permute-start | bytes 6291464 | tf_op jit(solution)/shard_map/ppermute | solution.py:17
  112.9 43.9 %collective-permute-done.5 = bf16[256,4096]{1,0:T(8,128)(2,1)} collective-permute-done((bf16[256,4096]{1,0:T(8,128)(2,1)S(1)}, bf16[256,4096]{1,0:T(8,128)(2,1)}, u32[]{:S(2)}, u32[]{:S(2)}) %collective-permute-start.5) | collective-permute-done | bytes 2097184 | tf_op jit(solution)/shard_map/ppermute | solution.py:15
  156.8 0.0 copy-done.3
  156.8 0.1 collective-permute-start.7
  156.9 2.8 fusion.28
  159.7 0.0 copy-done.8
  159.7 0.0 collective-permute-done.4
  159.7 5.4 %collective-permute-start.6 = (bf16[256,4096]{1,0:T(8,128)(2,1)}, bf16[256,4096]{1,0:T(8,128)(2,1)}, u32[]{:S(2)}, u32[]{:S(2)}) collective-permute-start(bf16[256,4096]{1,0:T(8,128)(2,1)} %collective-permute-done.4), channel_id=1, source_target_pairs={{0,240},{16,0},{32,16},{48,32},{64,48},{80,64},{96,80},{112,96},{1... | collective-permute-start | bytes 6291464 | tf_op jit(solution)/shard_map/ppermute | solution.py:17
  165.1 3.1 fusion.20
  168.2 0.0 all-reduce.2.cloned.1.call-update
  168.3 37.2 %collective-permute-done.7 = bf16[256,4096]{1,0:T(8,128)(2,1)} collective-permute-done((bf16[256,4096]{1,0:T(8,128)(2,1)}, bf16[256,4096]{1,0:T(8,128)(2,1)}, u32[]{:S(2)}, u32[]{:S(2)}) %collective-permute-start.7) | collective-permute-done | bytes 2097184 | tf_op jit(solution)/shard_map/ppermute | solution.py:15
  205.5 0.0 collective-permute-start.9
  205.5 0.0 copy-done.5
  205.5 2.4 fusion.16
  207.9 3.0 copy.11
  211.0 27.9 %psum.15 = f32[1,32,128]{2,1,0:T(8,128)S(1)} all-reduce(f32[1,32,128]{2,1,0:T(8,128)S(1)} %bitcast.120), channel_id=1, replica_groups=mesh['dp'=16,'sp'=8,'shift'=2] {'sp'}, use_global_device_ids=true, to_apply=%region_2.3 | all-reduce | flops 4096 | bytes 32768 | tf_op jit(solution)/shard_map/psum | solution.py:50
  238.9 0.9 fusion.86
  239.8 0.0 collective-permute-done.6
  239.8 5.5 %collective-permute-start.8 = (bf16[256,4096]{1,0:T(8,128)(2,1)}, bf16[256,4096]{1,0:T(8,128)(2,1)}, u32[]{:S(2)}, u32[]{:S(2)}) collective-permute-start(bf16[256,4096]{1,0:T(8,128)(2,1)} %collective-permute-done.6), channel_id=1, source_target_pairs={{0,240},{16,0},{32,16},{48,32},{64,48},{80,64},{96,80},{112,96},{1... | collective-permute-start | bytes 6291464 | tf_op jit(solution)/shard_map/ppermute | solution.py:17
  245.3 2.5 fusion.15
  247.8 5.4 %collective-permute-done.9 = bf16[256,4096]{1,0:T(8,128)(2,1)} collective-permute-done((bf16[256,4096]{1,0:T(8,128)(2,1)}, bf16[256,4096]{1,0:T(8,128)(2,1)}, u32[]{:S(2)}, u32[]{:S(2)}) %collective-permute-start.9) | collective-permute-done | bytes 2097184 | tf_op jit(solution)/shard_map/ppermute | solution.py:15
  253.2 0.0 collective-permute-start.11
  253.2 0.7 fusion.50
  253.9 0.8 copy-done.11
  254.8 0.8 convolution_add_fusion.8
  255.6 0.8 copy-done.7
  256.4 0.7 convolution_add_fusion.7
  257.1 0.8 copy-done.4
  258.0 0.7 fusion.45
  258.7 27.0 %collective-permute-done.8 = bf16[256,4096]{1,0:T(8,128)(2,1)} collective-permute-done((bf16[256,4096]{1,0:T(8,128)(2,1)}, bf16[256,4096]{1,0:T(8,128)(2,1)}, u32[]{:S(2)}, u32[]{:S(2)}) %collective-permute-start.8) | collective-permute-done | bytes 2097184 | tf_op jit(solution)/shard_map/ppermute | solution.py:17
  285.7 5.4 %collective-permute-start.10 = (bf16[256,4096]{1,0:T(8,128)(2,1)}, bf16[256,4096]{1,0:T(8,128)(2,1)S(1)}, u32[]{:S(2)}, u32[]{:S(2)}) collective-permute-start(bf16[256,4096]{1,0:T(8,128)(2,1)} %collective-permute-done.8), channel_id=1, source_target_pairs={{0,240},{16,0},{32,16},{48,32},{64,48},{80,64},{96,80},{112,96},{1... | collective-permute-start | bytes 6291464 | tf_op jit(solution)/shard_map/ppermute | solution.py:17
  291.1 0.8 fusion.5
  291.9 8.1 %collective-permute-done.11 = bf16[256,4096]{1,0:T(8,128)(2,1)S(1)} collective-permute-done((bf16[256,4096]{1,0:T(8,128)(2,1)}, bf16[256,4096]{1,0:T(8,128)(2,1)S(1)}, u32[]{:S(2)}, u32[]{:S(2)}) %collective-permute-start.11) | collective-permute-done | bytes 2097184 | tf_op jit(solution)/shard_map/ppermute | solution.py:15
  300.0 0.0 collective-permute-start.13
  300.0 2.3 fusion.42
  302.3 2.5 fusion.4
  304.8 2.3 fusion.39
  307.1 2.5 fusion.3
  309.6 22.1 %collective-permute-done.10 = bf16[256,4096]{1,0:T(8,128)(2,1)S(1)} collective-permute-done((bf16[256,4096]{1,0:T(8,128)(2,1)}, bf16[256,4096]{1,0:T(8,128)(2,1)S(1)}, u32[]{:S(2)}, u32[]{:S(2)}) %collective-permute-start.10) | collective-permute-done | bytes 2097184 | tf_op jit(solution)/shard_map/ppermute | solution.py:17
  331.7 5.4 %collective-permute-start.12 = (bf16[256,4096]{1,0:T(8,128)(2,1)S(1)}, bf16[256,4096]{1,0:T(8,128)(2,1)S(1)}, u32[]{:S(2)}, u32[]{:S(2)}) collective-permute-start(bf16[256,4096]{1,0:T(8,128)(2,1)S(1)} %collective-permute-done.10), channel_id=1, source_target_pairs={{0,240},{16,0},{32,16},{48,32},{64,48},{80,64},{96,80},{112,96},{1... | collective-permute-start | bytes 6291464 | tf_op jit(solution)/shard_map/ppermute | solution.py:17
  337.1 2.3 fusion.36
  339.4 6.3 %collective-permute-done.13 = bf16[256,4096]{1,0:T(8,128)(2,1)S(1)} collective-permute-done((bf16[256,4096]{1,0:T(8,128)(2,1)S(1)}, bf16[256,4096]{1,0:T(8,128)(2,1)S(1)}, u32[]{:S(2)}, u32[]{:S(2)}) %collective-permute-start.13) | collective-permute-done | bytes 2097184 | tf_op jit(solution)/shard_map/ppermute | solution.py:15
  345.8 0.0 collective-permute-start.14
  345.8 2.5 fusion.2
  348.2 0.7 fusion.33
  349.0 0.8 fusion.1
  349.8 0.7 fusion.30
  350.5 20.8 %collective-permute-done.12 = bf16[256,4096]{1,0:T(8,128)(2,1)S(1)} collective-permute-done((bf16[256,4096]{1,0:T(8,128)(2,1)S(1)}, bf16[256,4096]{1,0:T(8,128)(2,1)S(1)}, u32[]{:S(2)}, u32[]{:S(2)}) %collective-permute-start.12) | collective-permute-done | bytes 2097184 | tf_op jit(solution)/shard_map/ppermute | solution.py:17
  371.3 0.8 fusion
  372.0 18.6 %collective-permute-done.14 = bf16[256,4096]{1,0:T(8,128)(2,1)S(1)} collective-permute-done((bf16[256,4096]{1,0:T(8,128)(2,1)S(1)}, bf16[256,4096]{1,0:T(8,128)(2,1)S(1)}, u32[]{:S(2)}, u32[]{:S(2)}) %collective-permute-start.14) | collective-permute-done | bytes 2097184 | tf_op jit(solution)/shard_map/ppermute | solution.py:15
  390.6 2.1 fusion.7
  (18 shorter events, 0.0 us)
Async XLA Ops:
  6.5 158.6 %copy-start = (bf16[1,256,32,128]{3,2,1,0:T(8,128)(2,1)S(1)}, bf16[1,256,32,128]{3,2,1,0:T(8,128)(2,1)}, u32[]{:S(2)}) copy-start(bf16[1,256,32,128]{3,2,1,0:T(8,128)(2,1)} %param.6) | copy-start | bytes 6291460
  6.5 238.8 %all-reduce.2.cloned.1.call-start = ((), (), s32[]{:S(2)}) async-start(), calls=%async_computation | async-start | bytes 4194304 | tf_op jit(solution)/shard_map/psum | solution.py:50
  6.5 51.0 %collective-permute-start.1 = (bf16[256,4096]{1,0:T(8,128)(2,1)}, bf16[256,4096]{1,0:T(8,128)(2,1)S(1)}, u32[]{:S(2)}, u32[]{:S(2)}) collective-permute-start(bf16[256,4096]{1,0:T(8,128)(2,1)} %param.7), channel_id=1, source_target_pairs={{0,16},{16,32},{32,48},{48,64},{64,80},{80,96},{96,112},{112,128},... | collective-permute-start | bytes 6291464 | tf_op jit(solution)/shard_map/ppermute | solution.py:15
  8.0 49.6 %collective-permute-start = (bf16[256,4096]{1,0:T(8,128)(2,1)}, bf16[256,4096]{1,0:T(8,128)(2,1)S(1)}, u32[]{:S(2)}, u32[]{:S(2)}) collective-permute-start(bf16[256,4096]{1,0:T(8,128)(2,1)} %param.7), channel_id=1, source_target_pairs={{0,240},{16,0},{32,16},{48,32},{64,48},{80,64},{96,80},{112,96},{1... | collective-permute-start | bytes 6291464 | tf_op jit(solution)/shard_map/ppermute | solution.py:17
  57.6 99.2 %copy-start.6 = (bf16[256,4096]{1,0:T(8,128)(2,1)}, bf16[256,4096]{1,0:T(8,128)(2,1)S(1)}, u32[]{:S(2)}) copy-start(bf16[256,4096]{1,0:T(8,128)(2,1)S(1)} %collective-permute-done.1) | copy-start | bytes 6291460
  57.6 50.0 %collective-permute-start.3 = (bf16[256,4096]{1,0:T(8,128)(2,1)S(1)}, bf16[256,4096]{1,0:T(8,128)(2,1)S(1)}, u32[]{:S(2)}, u32[]{:S(2)}) collective-permute-start(bf16[256,4096]{1,0:T(8,128)(2,1)S(1)} %collective-permute-done.1), channel_id=1, source_target_pairs={{0,16},{16,32},{32,48},{48,64},{64,80},{80,96},{96,112},{112,128},... | collective-permute-start | bytes 6291464 | tf_op jit(solution)/shard_map/ppermute | solution.py:15
  57.6 99.2 %copy-start.10 = (bf16[256,4096]{1,0:T(8,128)(2,1)}, bf16[256,4096]{1,0:T(8,128)(2,1)S(1)}, u32[]{:S(2)}) copy-start(bf16[256,4096]{1,0:T(8,128)(2,1)S(1)} %collective-permute-done) | copy-start | bytes 6291460
  57.6 50.0 %collective-permute-start.2 = (bf16[256,4096]{1,0:T(8,128)(2,1)S(1)}, bf16[256,4096]{1,0:T(8,128)(2,1)S(1)}, u32[]{:S(2)}, u32[]{:S(2)}) collective-permute-start(bf16[256,4096]{1,0:T(8,128)(2,1)S(1)} %collective-permute-done), channel_id=1, source_target_pairs={{0,240},{16,0},{32,16},{48,32},{64,48},{80,64},{96,80},{112,96},{1... | collective-permute-start | bytes 6291464 | tf_op jit(solution)/shard_map/ppermute | solution.py:17
  107.6 49.2 %copy-start.3 = (bf16[256,4096]{1,0:T(8,128)(2,1)}, bf16[256,4096]{1,0:T(8,128)(2,1)S(1)}, u32[]{:S(2)}) copy-start(bf16[256,4096]{1,0:T(8,128)(2,1)S(1)} %collective-permute-done.3) | copy-start | bytes 6291460
  107.6 49.2 %collective-permute-start.5 = (bf16[256,4096]{1,0:T(8,128)(2,1)S(1)}, bf16[256,4096]{1,0:T(8,128)(2,1)}, u32[]{:S(2)}, u32[]{:S(2)}) collective-permute-start(bf16[256,4096]{1,0:T(8,128)(2,1)S(1)} %collective-permute-done.3), channel_id=1, source_target_pairs={{0,16},{16,32},{32,48},{48,64},{64,80},{80,96},{96,112},{112,128},... | collective-permute-start | bytes 6291464 | tf_op jit(solution)/shard_map/ppermute | solution.py:15
  107.6 52.1 %copy-start.8 = (bf16[256,4096]{1,0:T(8,128)(2,1)}, bf16[256,4096]{1,0:T(8,128)(2,1)S(1)}, u32[]{:S(2)}) copy-start(bf16[256,4096]{1,0:T(8,128)(2,1)S(1)} %collective-permute-done.2) | copy-start | bytes 6291460
  107.6 52.1 %collective-permute-start.4 = (bf16[256,4096]{1,0:T(8,128)(2,1)S(1)}, bf16[256,4096]{1,0:T(8,128)(2,1)}, u32[]{:S(2)}, u32[]{:S(2)}) collective-permute-start(bf16[256,4096]{1,0:T(8,128)(2,1)S(1)} %collective-permute-done.2), channel_id=1, source_target_pairs={{0,240},{16,0},{32,16},{48,32},{64,48},{80,64},{96,80},{112,96},{1... | collective-permute-start | bytes 6291464 | tf_op jit(solution)/shard_map/ppermute | solution.py:17
  156.8 48.7 %collective-permute-start.7 = (bf16[256,4096]{1,0:T(8,128)(2,1)}, bf16[256,4096]{1,0:T(8,128)(2,1)}, u32[]{:S(2)}, u32[]{:S(2)}) collective-permute-start(bf16[256,4096]{1,0:T(8,128)(2,1)} %collective-permute-done.5), channel_id=1, source_target_pairs={{0,16},{16,32},{32,48},{48,64},{64,80},{80,96},{96,112},{112,128},... | collective-permute-start | bytes 6291464 | tf_op jit(solution)/shard_map/ppermute | solution.py:15
  159.7 80.1 %collective-permute-start.6 = (bf16[256,4096]{1,0:T(8,128)(2,1)}, bf16[256,4096]{1,0:T(8,128)(2,1)}, u32[]{:S(2)}, u32[]{:S(2)}) collective-permute-start(bf16[256,4096]{1,0:T(8,128)(2,1)} %collective-permute-done.4), channel_id=1, source_target_pairs={{0,240},{16,0},{32,16},{48,32},{64,48},{80,64},{96,80},{112,96},{1... | collective-permute-start | bytes 6291464 | tf_op jit(solution)/shard_map/ppermute | solution.py:17
  168.2 37.2 %copy-start.5 = (bf16[1,256,32,128]{3,2,1,0:T(8,128)(2,1)S(1)}, bf16[1,256,32,128]{3,2,1,0:T(8,128)(2,1)}, u32[]{:S(2)}) copy-start(bf16[1,256,32,128]{3,2,1,0:T(8,128)(2,1)} %param.4) | copy-start | bytes 6291460
  205.5 47.7 %collective-permute-start.9 = (bf16[256,4096]{1,0:T(8,128)(2,1)}, bf16[256,4096]{1,0:T(8,128)(2,1)}, u32[]{:S(2)}, u32[]{:S(2)}) collective-permute-start(bf16[256,4096]{1,0:T(8,128)(2,1)} %collective-permute-done.7), channel_id=1, source_target_pairs={{0,16},{16,32},{32,48},{48,64},{64,80},{80,96},{96,112},{112,128},... | collective-permute-start | bytes 6291464 | tf_op jit(solution)/shard_map/ppermute | solution.py:15
  239.8 45.9 %collective-permute-start.8 = (bf16[256,4096]{1,0:T(8,128)(2,1)}, bf16[256,4096]{1,0:T(8,128)(2,1)}, u32[]{:S(2)}, u32[]{:S(2)}) collective-permute-start(bf16[256,4096]{1,0:T(8,128)(2,1)} %collective-permute-done.6), channel_id=1, source_target_pairs={{0,240},{16,0},{32,16},{48,32},{64,48},{80,64},{96,80},{112,96},{1... | collective-permute-start | bytes 6291464 | tf_op jit(solution)/shard_map/ppermute | solution.py:17
  245.3 7.9 %copy-start.2 = (bf16[256,4096]{1,0:T(8,128)(2,1)S(1)}, bf16[256,4096]{1,0:T(8,128)(2,1)}, u32[]{:S(2)}) copy-start(bf16[256,4096]{1,0:T(8,128)(2,1)} %param.7) | copy-start | bytes 6291460
  253.2 46.8 %collective-permute-start.11 = (bf16[256,4096]{1,0:T(8,128)(2,1)}, bf16[256,4096]{1,0:T(8,128)(2,1)S(1)}, u32[]{:S(2)}, u32[]{:S(2)}) collective-permute-start(bf16[256,4096]{1,0:T(8,128)(2,1)} %collective-permute-done.9), channel_id=1, source_target_pairs={{0,16},{16,32},{32,48},{48,64},{64,80},{80,96},{96,112},{112,128},... | collective-permute-start | bytes 6291464 | tf_op jit(solution)/shard_map/ppermute | solution.py:15
  253.2 1.6 copy-start.11
  254.8 1.6 copy-start.7
  256.4 1.6 copy-start.4
  258.0 33.1 %copy-start.9 = (bf16[256,4096]{1,0:T(8,128)(2,1)S(1)}, bf16[256,4096]{1,0:T(8,128)(2,1)}, u32[]{:S(2)}) copy-start(bf16[256,4096]{1,0:T(8,128)(2,1)} %copy-done.8) | copy-start | bytes 6291460
  285.7 46.0 %collective-permute-start.10 = (bf16[256,4096]{1,0:T(8,128)(2,1)}, bf16[256,4096]{1,0:T(8,128)(2,1)S(1)}, u32[]{:S(2)}, u32[]{:S(2)}) collective-permute-start(bf16[256,4096]{1,0:T(8,128)(2,1)} %collective-permute-done.8), channel_id=1, source_target_pairs={{0,240},{16,0},{32,16},{48,32},{64,48},{80,64},{96,80},{112,96},{1... | collective-permute-start | bytes 6291464 | tf_op jit(solution)/shard_map/ppermute | solution.py:17
  300.0 45.8 %collective-permute-start.13 = (bf16[256,4096]{1,0:T(8,128)(2,1)S(1)}, bf16[256,4096]{1,0:T(8,128)(2,1)S(1)}, u32[]{:S(2)}, u32[]{:S(2)}) collective-permute-start(bf16[256,4096]{1,0:T(8,128)(2,1)S(1)} %collective-permute-done.11), channel_id=1, source_target_pairs={{0,16},{16,32},{32,48},{48,64},{64,80},{80,96},{96,112},{112,128},... | collective-permute-start | bytes 6291464 | tf_op jit(solution)/shard_map/ppermute | solution.py:15
  331.7 39.5 %collective-permute-start.12 = (bf16[256,4096]{1,0:T(8,128)(2,1)S(1)}, bf16[256,4096]{1,0:T(8,128)(2,1)S(1)}, u32[]{:S(2)}, u32[]{:S(2)}) collective-permute-start(bf16[256,4096]{1,0:T(8,128)(2,1)S(1)} %collective-permute-done.10), channel_id=1, source_target_pairs={{0,240},{16,0},{32,16},{48,32},{64,48},{80,64},{96,80},{112,96},{1... | collective-permute-start | bytes 6291464 | tf_op jit(solution)/shard_map/ppermute | solution.py:17
  345.8 44.8 %collective-permute-start.14 = (bf16[256,4096]{1,0:T(8,128)(2,1)S(1)}, bf16[256,4096]{1,0:T(8,128)(2,1)S(1)}, u32[]{:S(2)}, u32[]{:S(2)}) collective-permute-start(bf16[256,4096]{1,0:T(8,128)(2,1)S(1)} %collective-permute-done.13), channel_id=1, source_target_pairs={{0,16},{16,32},{32,48},{48,64},{64,80},{80,96},{96,112},{112,128},... | collective-permute-start | bytes 6291464 | tf_op jit(solution)/shard_map/ppermute | solution.py:15
  390.6 2.1 copy-start.1
Sparse Core Ops, SparseCore 0:
  168.4 76.2 all-reduce.1
